TPU v7x, 256 devices: a whole 4x4x8 slice. The times are simulated.
256 devices in a mesh: stage: 64 (over z, y, core), expert: 4 (over x).
Axes of the slice: x: 4, y: 4, z: 8, core: 2. Of those that a mesh axis runs over, the one named last changes fastest.
Arguments:
- x_act: bfloat16 [64, 8192, 128], P('stage', 'expert')
- route_idx: int32 [64, 8192, 4], P('stage', 'expert')
- route_wts: float32 [64, 8192, 4], P('stage', 'expert')
- w_one: bfloat16 [64, 16, 128, 512], P('stage', 'expert')
- w_three: bfloat16 [64, 16, 128, 512], P('stage', 'expert')
- w_two: bfloat16 [64, 16, 512, 128], P('stage', 'expert')
- dy_act: bfloat16 [64, 8192, 128], P('stage', 'expert')
Outputs:
- output 1: bfloat16 [64, 8192, 128], P('stage', 'expert')
- output 2: bfloat16 [64, 8192, 128], P('stage', 'expert')
- output 3: bfloat16 [64, 16, 128, 512], P('stage', 'expert')
- output 4: bfloat16 [64, 16, 128, 512], P('stage', 'expert')
- output 5: bfloat16 [64, 16, 512, 128], P('stage', 'expert')
All inputs are finite; a program needn't handle non-finite values.
Results may differ from a plain program's by a relative error of at most 0.0125934.
Values are sent between devices in bfloat16 or wider.
A program may use at most 768 MiB of HBM per device.

v0:
```python
import jax
import jax.numpy as jnp
from jax import lax
from jax.sharding import PartitionSpec as P


def slot_tables(idx_blk, first_exp, n_exp, capacity):
    n_slot = idx_blk.shape[0] * idx_blk.shape[1]
    slot_ids = idx_blk.reshape(n_slot) - first_exp
    hit_mat = (slot_ids[:, None] == jnp.arange(n_exp, dtype=jnp.int32)[None, :]).astype(jnp.int32)
    slot_rank = jnp.sum(jnp.cumsum(hit_mat, axis=0) * hit_mat, axis=1) - 1
    is_local = (slot_ids >= 0) & (slot_ids < n_exp)
    buf_pos = jnp.where(is_local, slot_ids * capacity + slot_rank, n_exp * capacity)
    slot_at = jnp.full((n_exp * capacity,), n_slot, jnp.int32).at[buf_pos].set(jnp.arange(n_slot, dtype=jnp.int32), mode='drop')
    return buf_pos, slot_at


def take_rows(row_table, row_ids):
    return jnp.take(row_table, row_ids, axis=0, mode='fill', fill_value=0)


def expert_forward(x_buf, w_in_one, w_in_three, w_out):
    pre_one = jnp.einsum('pecd,edf->pecf', x_buf, w_in_one, preferred_element_type=jnp.float32)
    pre_three = jnp.einsum('pecd,edf->pecf', x_buf, w_in_three, preferred_element_type=jnp.float32)
    hidden = (pre_one * jax.nn.sigmoid(pre_one) * pre_three).astype(jnp.bfloat16)
    return jnp.einsum('pecf,efd->pecd', hidden, w_out, preferred_element_type=jnp.float32).astype(jnp.bfloat16)


def expert_backward(x_buf, d_buf, w_in_one, w_in_three, w_out):
    pre_one = jnp.einsum('pecd,edf->pecf', x_buf, w_in_one, preferred_element_type=jnp.float32)
    pre_three = jnp.einsum('pecd,edf->pecf', x_buf, w_in_three, preferred_element_type=jnp.float32)
    sig_one = jax.nn.sigmoid(pre_one)
    act_one = pre_one * sig_one
    hidden = (act_one * pre_three).astype(jnp.bfloat16)
    d_hidden = jnp.einsum('pecd,efd->pecf', d_buf, w_out, preferred_element_type=jnp.float32).astype(jnp.bfloat16).astype(jnp.float32)
    d_three = (d_hidden * act_one).astype(jnp.bfloat16)
    d_one = (d_hidden * pre_three * sig_one * (1.0 + pre_one * (1.0 - sig_one))).astype(jnp.bfloat16)
    dx_buf = (jnp.einsum('pecf,edf->pecd', d_one, w_in_one, preferred_element_type=jnp.float32) + jnp.einsum('pecf,edf->pecd', d_three, w_in_three, preferred_element_type=jnp.float32)).astype(jnp.bfloat16)
    g_one = jnp.einsum('pecd,pecf->edf', x_buf, d_one, preferred_element_type=jnp.float32).astype(jnp.bfloat16)
    g_three = jnp.einsum('pecd,pecf->edf', x_buf, d_three, preferred_element_type=jnp.float32).astype(jnp.bfloat16)
    g_two = jnp.einsum('pecf,pecd->efd', hidden, d_buf, preferred_element_type=jnp.float32).astype(jnp.bfloat16)
    return dx_buf, g_one, g_three, g_two


def solution(mesh):
    n_stage = mesh.shape['stage']
    n_dev = mesh.shape['expert']
    to_next = [(stage_idx, (stage_idx + 1) % n_stage) for stage_idx in range(n_stage)]
    to_prev = [((stage_idx + 1) % n_stage, stage_idx) for stage_idx in range(n_stage)]
    tok_spec = P('stage', 'expert', None)
    w_spec = P('stage', 'expert', None, None)

    def moe_layer(x_act, route_idx, route_wts, w_one, w_three, w_two, dy_act):
        x_src = x_act[0]
        n_tok, model_dim = x_src.shape
        top_k = route_idx.shape[2]
        n_local = w_one.shape[1]
        n_exp = n_local * n_dev
        capacity = 2 * n_tok * top_k // n_exp - 1
        w_in_one, w_in_three, w_out = w_one[0], w_three[0], w_two[0]

        x_dst = lax.ppermute(x_src, 'stage', to_next)
        idx_dst = lax.ppermute(route_idx[0], 'stage', to_next)
        wts_dst = lax.ppermute(route_wts[0], 'stage', to_next)
        buf_pos, slot_at = slot_tables(idx_dst, 0, n_exp, capacity)

        def dispatch(row_src, row_ids):
            send_buf = take_rows(row_src, row_ids).reshape(n_dev, n_local, capacity, model_dim)
            return lax.all_to_all(send_buf, 'expert', 0, 0)

        def combine(buf_rows):
            back_buf = lax.all_to_all(buf_rows, 'expert', 0, 0).reshape(n_exp * capacity, model_dim)
            return take_rows(back_buf, buf_pos).reshape(n_tok, top_k, model_dim)

        out_slot = combine(expert_forward(dispatch(x_dst, slot_at // top_k), w_in_one, w_in_three, w_out))
        y_dst = jnp.sum(wts_dst[:, :, None] * out_slot.astype(jnp.float32), axis=1).astype(jnp.bfloat16)

        x_again, y_dst = lax.optimization_barrier((x_src, y_dst))
        x_dst = lax.ppermute(x_again, 'stage', to_next)
        d_slot = (wts_dst[:, :, None] * dy_act[0][:, None, :].astype(jnp.float32)).astype(jnp.bfloat16).reshape(n_tok * top_k, model_dim)
        dx_buf, g_one, g_three, g_two = expert_backward(dispatch(x_dst, slot_at // top_k), dispatch(d_slot, slot_at), w_in_one, w_in_three, w_out)
        dx_slot = combine(dx_buf)
        dx_dst = jnp.sum(dx_slot.astype(jnp.float32), axis=1).astype(jnp.bfloat16)
        dx_src = lax.ppermute(dx_dst, 'stage', to_prev)
        return y_dst[None], dx_src[None], g_one[None], g_three[None], g_two[None]

    return jax.shard_map(moe_layer, mesh=mesh, in_specs=(tok_spec, tok_spec, tok_spec, w_spec, w_spec, w_spec, tok_spec), out_specs=(tok_spec, tok_spec, w_spec, w_spec, w_spec), check_vma=False)
```

profile of v0, /device:TPU:113, one launch (start us, length us, event | category | flops | bytes accessed | tf_op | source)
XLA Modules:
  0.0 759.6 jit_solution(1726880920041523259)
XLA Ops:
  0.6 1.6 collective-permute-start.2
  2.4 0.9 collective-permute-done.2
  3.7 0.6 eq.25
  4.3 0.6 eq.29
  5.0 0.5 copy.34
  5.5 0.8 and.35
  6.3 4.8 reduce-window.6
  11.1 0.5 slice_reduce_fusion
  12.0 0.4 fusion.51
  12.9 0.7 mul.79
  13.7 30.9 %scatter_custom_fusion = s32[16368]{0:T(1024)S(1)} fusion(s32[8192]{0:T(1024)S(1)} %bitcast.182, s32[8192]{0:T(1024)S(1)} %iota.11, s32[]{:T(128)} %constant.44.clone.1), kind=kCustom, calls=%fused_computation.92 | custom fusion | bytes 65476 | tf_op jit(solution)/shard_map/scatter | solution.py:14
  44.8 57.9 %gather_fusion.1 = bf16[16368,128]{1,0:T(8,128)(2,1)} fusion(bf16[2048,128]{1,0:T(8,128)(2,1)S(1)} %collective-permute-done.1, s32[16384]{0:T(1024)S(1)} %pad_clamp_fusion.1), kind=kCustom, calls=%fused_computation.clone | custom fusion | bytes 8445888 | tf_op jit(solution)/shard_map/jit(_take)/gather | solution.py:19
  102.7 12.0 %broadcast_select_fusion.2 = bf16[16368,128]{1,0:T(8,128)(2,1)} fusion(bf16[16368,128]{1,0:T(8,128)(2,1)} %gather_fusion.1, pred[16368]{0:T(1024)(128)(4,1)S(1)} %get-tuple-element.11), kind=kLoop, calls=%fused_computation.40 | loop fusion | flops 2095104 | bytes 8396784 | tf_op jit(solution)/shard_map/jit(_take)/select_n | solution.py:19
  114.7 4.2 reshape.144
  118.8 5.4 copy.36
  124.3 51.3 %all_to_all.25 = bf16[4,4,1023,128]{3,1,2,0:T(4,128)(2,1)S(1)} all-to-all(bf16[4,4,1023,128]{3,1,2,0:T(4,128)(2,1)S(1)} %copy.36), channel_id=1, replica_groups=mesh['stage'=64,'expert'=4] {'expert'}, dimensions={0} | all-to-all | bytes 8380416 | tf_op jit(solution)/shard_map/all_to_all | solution.py:69
  175.5 2.0 copy-done.4
  177.5 13.1 %fusion.25 = f32[4,4,1023,512]{3,2,1,0:T(8,128)} fusion(bf16[4,4,1023,128]{3,1,2,0:T(4,128)(2,1)S(1)} %all_to_all.25, bf16[1,4,128,512]{3,2,1,0:T(8,128)(2,1)S(1)} %copy-done.5), kind=kOutput, calls=%fused_computation.44 | convolution fusion | flops 2145386496 | bytes 38236160 | tf_op jit(solution)/shard_map/pecd,edf->pecf/dot_general | solution.py:23
  190.6 20.0 %convert_bitcast_fusion = bf16[4,4,1023,128]{3,2,0,1:T(8,128)(2,1)} fusion(f32[4,4,1023,512]{3,2,1,0:T(8,128)} %fusion.25, bf16[4,4,1023,128]{3,1,2,0:T(4,128)(2,1)} %copy-done.4, bf16[1,4,128,512]{3,2,1,0:T(8,128)(2,1)S(1)} %copy-done.7, bf16[1,4,512,128]{3,2,1,0:T(8,128)(2,1)S(1)} %copy-done), kind=kOutput, calls=%fused_computation.37 | convolution fusion | flops 4343150592 | bytes 42950656 | tf_op jit(solution)/shard_map/pecf,efd->pecd/dot_general | solution.py:26
  210.5 7.4 copy.39
  217.9 5.0 all-to-all-start.1
  222.9 5.3 collective-permute-start
  228.2 1.0 collective-permute-done
  229.6 39.3 %all-to-all-done.1 = bf16[4,4,1023,128]{3,1,2,0:T(4,128)(2,1)} async-done(((bf16[4,4,1023,128]{3,1,2,0:T(4,128)(2,1)}), bf16[4,4,1023,128]{3,1,2,0:T(4,128)(2,1)}, u32[]{:S(2)}, u32[]{:S(2)}) %all-to-all-start.1) | async-done | bytes 4190240 | tf_op jit(solution)/shard_map/all_to_all | solution.py:72
  268.9 4.9 copy.40
  273.7 4.2 reshape.145
  277.9 30.9 %gather_fusion.2 = bf16[8192,128]{1,0:T(8,128)(2,1)} fusion(bf16[16368,128]{1,0:T(8,128)(2,1)} %reshape.145, s32[8192]{0:T(1024)S(1)} %get-tuple-element.16), kind=kCustom, calls=%fused_computation.1.clone | custom fusion | bytes 4227072 | tf_op jit(solution)/shard_map/jit(_take)/gather | solution.py:19
  308.8 5.9 broadcast_select_fusion.4
  314.7 12.1 %fusion.20 = bf16[2048,128]{1,0:T(8,128)(2,1)} fusion(bf16[2048,4,128]{2,1,0:T(4,128)(2,1)S(1)} %bitcast.175, f32[2048,4]{1,0:T(8,128)S(1)} %copy.31), kind=kLoop, calls=%fused_computation.35 | loop fusion | flops 2883584 | bytes 2654208 | tf_op jit(solution)/shard_map/reduce_sum | solution.py:76
  326.8 7.6 collective-permute-start.3
  334.4 6.1 collective-permute-done.3
  340.5 57.9 %gather_fusion.3 = bf16[16368,128]{1,0:T(8,128)(2,1)} fusion(bf16[2048,128]{1,0:T(8,128)(2,1)S(1)} %collective-permute-done.3, s32[16384]{0:T(1024)S(1)} %pad_clamp_fusion.1), kind=kCustom, calls=%fused_computation.2.clone | custom fusion | bytes 8445888 | tf_op jit(solution)/shard_map/jit(_take)/gather | solution.py:19
  398.4 12.0 %broadcast_select_fusion.1 = bf16[16368,128]{1,0:T(8,128)(2,1)} fusion(bf16[16368,128]{1,0:T(8,128)(2,1)} %gather_fusion.3, pred[16368]{0:T(1024)(128)(4,1)S(1)} %get-tuple-element.11), kind=kLoop, calls=%fused_computation.39 | loop fusion | flops 2095104 | bytes 8396784 | tf_op jit(solution)/shard_map/jit(_take)/select_n | solution.py:19
  410.4 4.2 reshape.146
  414.5 7.4 copy.44
  421.9 5.4 all-to-all-start.3
  427.4 0.6 mul.86
  428.2 0.8 mul.88
  429.0 3.5 multiply_convert_fusion
  432.5 57.8 %gather_fusion = bf16[16368,128]{1,0:T(8,128)(2,1)} fusion(bf16[8192,128]{1,0:T(8,128)(2,1)S(1)} %multiply_convert_fusion, s32[16384]{0:T(1024)S(1)} %pad_clamp_fusion), kind=kCustom, calls=%fused_computation.4 | custom fusion | bytes 8445888 | tf_op jit(solution)/shard_map/jit(_take)/gather | solution.py:19
  490.3 4.2 gather.13
  494.5 6.1 broadcast_select_fusion
  500.6 5.2 copy.42
  505.8 5.0 all-to-all-start.2
  510.8 7.5 copy.49
  518.3 18.1 %fusion.54 = f32[4,4,1023,512]{3,2,1,0:T(8,128)} fusion(bf16[4,4,1023,128]{2,3,0,1:T(8,128)(2,1)} %copy.49, bf16[1,4,128,512]{3,2,1,0:T(8,128)(2,1)} %param.14), kind=kOutput, calls=%fused_computation.64 | convolution fusion | flops 2145386496 | bytes 38236160 | tf_op jit(solution)/shard_map/pecd,edf->pecf/dot_general | solution.py:30
  536.4 14.2 %fusion.58 = f32[4,4,1023,512]{3,2,1,0:T(8,128)} fusion(bf16[4,4,1023,128]{2,3,0,1:T(8,128)(2,1)S(1)} %copy-done.2, bf16[1,4,128,512]{3,2,1,0:T(8,128)(2,1)} %param.15), kind=kOutput, calls=%fused_computation.68 | convolution fusion | flops 2145386496 | bytes 38236160 | tf_op jit(solution)/shard_map/pecd,edf->pecf/dot_general | solution.py:31
  550.6 8.3 %all-to-all-done.2 = bf16[4,4,1023,128]{3,1,2,0:T(4,128)(2,1)} async-done(((bf16[4,4,1023,128]{3,1,2,0:T(4,128)(2,1)}), bf16[4,4,1023,128]{3,1,2,0:T(4,128)(2,1)}, u32[]{:S(2)}, u32[]{:S(2)}) %all-to-all-start.2) | async-done | bytes 4190240 | tf_op jit(solution)/shard_map/all_to_all | solution.py:69
  558.9 39.3 %fusion.8 = (bf16[4,4,1023,512]{3,2,0,1:T(8,128)(2,1)}, bf16[4,4,1023,512]{3,2,0,1:T(8,128)(2,1)}) fusion(f32[4,4,1023,512]{3,2,1,0:T(8,128)} %fusion.54, f32[4,4,1023,512]{3,2,1,0:T(8,128)} %fusion.58, bf16[1,4,512,128]{3,2,1,0:T(8,128)(2,1)S(1)} %copy-done, bf16[4,4,1023,128]{3,1,2,0:T(4,128)(2,1)} %all-to-all-done.2), kind=kOutput, calls=%fused_computation.20 | convolution fusion | flops 2271092736 | bytes 105279488 | tf_op jit(solution)/shard_map/pecd,efd->pecf/dot_general | solution.py:35
  598.2 9.0 %fusion.48 = bf16[1,4,128,512]{3,2,1,0:T(8,128)(2,1)} fusion(bf16[4,4,1023,128]{2,3,0,1:T(8,128)(2,1)S(1)} %copy-done.3, bf16[4,4,1023,512]{3,2,0,1:T(8,128)(2,1)} %get-tuple-element.13), kind=kOutput, calls=%fused_computation.55 | convolution fusion | flops 2145648640 | bytes 21475328 | tf_op jit(solution)/shard_map/pecd,pecf->edf/dot_general | solution.py:40
  607.2 13.7 %fusion.52 = f32[4,4,1023,128]{3,2,1,0:T(8,128)} fusion(bf16[4,4,1023,512]{3,2,0,1:T(8,128)(2,1)} %get-tuple-element.14, bf16[1,4,128,512]{3,2,1,0:T(8,128)(2,1)S(1)} %copy-done.6), kind=kOutput, calls=%fused_computation.62 | convolution fusion | flops 2145386496 | bytes 25665536 | tf_op jit(solution)/shard_map/pecf,edf->pecd/dot_general | solution.py:38
  620.9 14.6 %fusion.19 = bf16[4,4,1023,128]{3,2,0,1:T(8,128)(2,1)} fusion(f32[4,4,1023,128]{3,2,1,0:T(8,128)} %fusion.52, bf16[4,4,1023,512]{3,2,0,1:T(8,128)(2,1)} %get-tuple-element.13, bf16[1,4,128,512]{3,2,1,0:T(8,128)(2,1)S(1)} %copy-done.8), kind=kOutput, calls=%fused_computation.33 | convolution fusion | flops 2149576704 | bytes 29855744 | tf_op jit(solution)/shard_map/pecf,edf->pecd/dot_general | solution.py:38
  635.5 7.4 copy.47
  642.9 5.0 all-to-all-start.4
  647.9 26.1 %fusion.43 = bf16[1,4,512,128]{3,2,1,0:T(8,128)(2,1)} fusion(bf16[4,4,1023,128]{3,1,2,0:T(4,128)(2,1)} %all-to-all-done.2, f32[4,4,1023,512]{3,2,1,0:T(8,128)} %fusion.58, f32[4,4,1023,512]{3,2,1,0:T(8,128)} %fusion.54), kind=kOutput, calls=%fused_computation.54 | convolution fusion | flops 2195931136 | bytes 71757824 | tf_op jit(solution)/shard_map/pecf,pecd->efd/dot_general | solution.py:41
  674.0 23.0 %all-to-all-done.4 = bf16[4,4,1023,128]{3,1,2,0:T(4,128)(2,1)} async-done(((bf16[4,4,1023,128]{3,1,2,0:T(4,128)(2,1)}), bf16[4,4,1023,128]{3,1,2,0:T(4,128)(2,1)}, u32[]{:S(2)}, u32[]{:S(2)}) %all-to-all-start.4) | async-done | bytes 4190240 | tf_op jit(solution)/shard_map/all_to_all | solution.py:72
  697.1 4.9 copy.48
  702.0 4.2 reshape.147
  706.2 24.6 %gather_fusion.4 = bf16[8192,128]{1,0:T(8,128)(2,1)S(1)} fusion(bf16[16368,128]{1,0:T(8,128)(2,1)} %reshape.147, s32[8192]{0:T(1024)S(1)} %copy-done.11), kind=kCustom, calls=%fused_computation.3.clone | custom fusion | bytes 4227072 | tf_op jit(solution)/shard_map/jit(_take)/gather | solution.py:19
  730.8 5.1 broadcast_select_fusion.3
  735.9 12.1 %reduce_sum.32 = bf16[2048,128]{1,0:T(8,128)(2,1)S(1)} reduce(bf16[2048,4,128]{2,1,0:T(4,128)(2,1)} %bitcast.176, bf16[]{:T(256)} %constant.73.clone.1), dimensions={1}, to_apply=%region_5.8 | reduce | flops 786432 | bytes 2621442 | tf_op jit(solution)/shard_map/reduce_sum | solution.py:83
  748.0 0.4 collective-permute-start.4
  748.3 10.2 %fusion.49 = bf16[1,4,128,512]{3,2,1,0:T(8,128)(2,1)} fusion(bf16[4,4,1023,128]{2,3,0,1:T(8,128)(2,1)} %copy.49, bf16[4,4,1023,512]{3,2,0,1:T(8,128)(2,1)} %get-tuple-element.14), kind=kOutput, calls=%fused_computation.56 | convolution fusion | flops 2145648640 | bytes 21475328 | tf_op jit(solution)/shard_map/pecd,pecf->edf/dot_general | solution.py:39
  758.6 0.8 copy.82
  (53 shorter events, 2.2 us)
Async XLA Ops:
  0.6 189.9 %copy-start = (bf16[1,4,512,128]{3,2,1,0:T(8,128)(2,1)S(1)}, bf16[1,4,512,128]{3,2,1,0:T(8,128)(2,1)}, u32[]{:S(2)}) copy-start(bf16[1,4,512,128]{3,2,1,0:T(8,128)(2,1)} %param.16) | copy-start | bytes 1572868
  0.6 2.7 collective-permute-start.2
  2.3 42.5 %collective-permute-start.1 = (bf16[2048,128]{1,0:T(8,128)(2,1)}, bf16[2048,128]{1,0:T(8,128)(2,1)S(1)}, u32[]{:S(2)}, u32[]{:S(2)}) collective-permute-start(bf16[2048,128]{1,0:T(8,128)(2,1)} %bitcast.183), channel_id=1, source_target_pairs={{0,4},{4,8},{8,12},{12,16},{16,20},{20,24},{24,28},{28,32},{32,36}... | collective-permute-start | bytes 1572872 | tf_op jit(solution)/shard_map/ppermute | solution.py:62
  12.5 265.5 %copy-start.10 = (s32[8192]{0:T(1024)}, s32[8192]{0:T(1024)S(1)}, u32[]{:S(2)}) copy-start(s32[8192]{0:T(1024)S(1)} %get-tuple-element.16) | copy-start | bytes 98308
  124.3 53.2 %copy-start.5 = (bf16[1,4,128,512]{3,2,1,0:T(8,128)(2,1)S(1)}, bf16[1,4,128,512]{3,2,1,0:T(8,128)(2,1)}, u32[]{:S(2)}) copy-start(bf16[1,4,128,512]{3,2,1,0:T(8,128)(2,1)} %param.14) | copy-start | bytes 1572868
  175.5 2.0 copy-start.4
  177.5 13.1 %copy-start.7 = (bf16[1,4,128,512]{3,2,1,0:T(8,128)(2,1)S(1)}, bf16[1,4,128,512]{3,2,1,0:T(8,128)(2,1)}, u32[]{:S(2)}) copy-start(bf16[1,4,128,512]{3,2,1,0:T(8,128)(2,1)} %param.15) | copy-start | bytes 1572868
  217.9 5.0 copy-start.15
  217.9 51.0 %all-to-all-start.1 = ((bf16[4,4,1023,128]{3,1,2,0:T(4,128)(2,1)}), bf16[4,4,1023,128]{3,1,2,0:T(4,128)(2,1)}, u32[]{:S(2)}, u32[]{:S(2)}) async-start(bf16[4,4,1023,128]{3,1,2,0:T(4,128)(2,1)} %copy.39), calls=%async_computation.1 | async-start | bytes 8380416 | tf_op jit(solution)/shard_map/all_to_all | solution.py:72
  222.9 6.3 collective-permute-start
  229.6 79.3 %copy-start.12 = (pred[8192]{0:T(1024)(128)(4,1)}, pred[8192]{0:T(1024)(128)(4,1)S(1)}, u32[]{:S(2)}) copy-start(pred[8192]{0:T(1024)(128)(4,1)S(1)} %compare_and_fusion.2) | copy-start | bytes 24580
  308.8 18.0 %copy-start.14 = (bf16[1,2048,128]{2,1,0:T(8,128)(2,1)S(1)}, bf16[1,2048,128]{2,1,0:T(8,128)(2,1)}, u32[]{:S(2)}) copy-start(bf16[1,2048,128]{2,1,0:T(8,128)(2,1)} %param.11) | copy-start | bytes 1572868
  326.8 13.7 %collective-permute-start.3 = (bf16[2048,128]{1,0:T(8,128)(2,1)S(1)}, bf16[2048,128]{1,0:T(8,128)(2,1)S(1)}, u32[]{:S(2)}, u32[]{:S(2)}) collective-permute-start(bf16[2048,128]{1,0:T(8,128)(2,1)S(1)} %bitcast.184), channel_id=1, source_target_pairs={{0,4},{4,8},{8,12},{12,16},{16,20},{20,24},{24,28},{28,32},{32,36}... | collective-permute-start | bytes 1572872 | tf_op jit(solution)/shard_map/ppermute | solution.py:79
  421.9 5.4 copy-start.9
  421.9 83.9 %all-to-all-start.3 = ((bf16[4,4,1023,128]{3,1,2,0:T(4,128)(2,1)}), bf16[4,4,1023,128]{3,1,2,0:T(4,128)(2,1)}, u32[]{:S(2)}, u32[]{:S(2)}) async-start(bf16[4,4,1023,128]{3,1,2,0:T(4,128)(2,1)} %copy.44), calls=%async_computation.3 | async-start | bytes 8380416 | tf_op jit(solution)/shard_map/all_to_all | solution.py:69
  505.8 53.1 %all-to-all-start.2 = ((bf16[4,4,1023,128]{3,1,2,0:T(4,128)(2,1)}), bf16[4,4,1023,128]{3,1,2,0:T(4,128)(2,1)}, u32[]{:S(2)}, u32[]{:S(2)}) async-start(bf16[4,4,1023,128]{3,1,2,0:T(4,128)(2,1)} %copy.42), calls=%async_computation.2 | async-start | bytes 8380416 | tf_op jit(solution)/shard_map/all_to_all | solution.py:69
  518.3 18.1 %copy-start.2 = (bf16[4,4,1023,128]{2,3,0,1:T(8,128)(2,1)S(1)}, bf16[4,4,1023,128]{2,3,0,1:T(8,128)(2,1)}, u32[]{:S(2)}) copy-start(bf16[4,4,1023,128]{2,3,0,1:T(8,128)(2,1)} %copy.49) | copy-start | bytes 12570628
  558.9 39.3 %copy-start.3 = (bf16[4,4,1023,128]{2,3,0,1:T(8,128)(2,1)S(1)}, bf16[4,4,1023,128]{2,3,0,1:T(8,128)(2,1)}, u32[]{:S(2)}) copy-start(bf16[4,4,1023,128]{2,3,0,1:T(8,128)(2,1)} %copy.49) | copy-start | bytes 12570628
  598.2 9.0 %copy-start.6 = (bf16[1,4,128,512]{3,2,1,0:T(8,128)(2,1)S(1)}, bf16[1,4,128,512]{3,2,1,0:T(8,128)(2,1)}, u32[]{:S(2)}) copy-start(bf16[1,4,128,512]{3,2,1,0:T(8,128)(2,1)} %param.14) | copy-start | bytes 1572868
  607.2 13.7 %copy-start.8 = (bf16[1,4,128,512]{3,2,1,0:T(8,128)(2,1)S(1)}, bf16[1,4,128,512]{3,2,1,0:T(8,128)(2,1)}, u32[]{:S(2)}) copy-start(bf16[1,4,128,512]{3,2,1,0:T(8,128)(2,1)} %param.15) | copy-start | bytes 1572868
  642.9 54.2 %all-to-all-start.4 = ((bf16[4,4,1023,128]{3,1,2,0:T(4,128)(2,1)}), bf16[4,4,1023,128]{3,1,2,0:T(4,128)(2,1)}, u32[]{:S(2)}, u32[]{:S(2)}) async-start(bf16[4,4,1023,128]{3,1,2,0:T(4,128)(2,1)} %copy.47), calls=%async_computation.4 | async-start | bytes 8380416 | tf_op jit(solution)/shard_map/all_to_all | solution.py:72
  702.0 4.2 copy-start.11
  706.2 24.6 %copy-start.13 = (pred[8192]{0:T(1024)(128)(4,1)S(1)}, pred[8192]{0:T(1024)(128)(4,1)}, u32[]{:S(2)}) copy-start(pred[8192]{0:T(1024)(128)(4,1)} %copy-done.12) | copy-start | bytes 24580
  748.0 10.6 %collective-permute-start.4 = (bf16[2048,128]{1,0:T(8,128)(2,1)S(1)}, bf16[2048,128]{1,0:T(8,128)(2,1)S(1)}, u32[]{:S(2)}, u32[]{:S(2)}) collective-permute-start(bf16[2048,128]{1,0:T(8,128)(2,1)S(1)} %reduce_sum.32), channel_id=1, source_target_pairs={{4,0},{8,4},{12,8},{16,12},{20,16},{24,20},{28,24},{32,28},{36,32}... | collective-permute-start | bytes 1572872 | tf_op jit(solution)/shard_map/ppermute | solution.py:84
  748.3 11.0 %copy-start.1 = (bf16[1,4,512,128]{3,2,1,0:T(8,128)(2,1)S(1)}, bf16[1,4,512,128]{3,2,1,0:T(8,128)(2,1)}, u32[]{:S(2)}) copy-start(bf16[1,4,512,128]{3,2,1,0:T(8,128)(2,1)} %param.16) | copy-start | bytes 1572868
where the time goes:
time: 767 us; the launch traced here: 760 us
  local copies, waits for them, and re-layouts  340 us (44%)
  matrix products  178 us (23%)
  waiting for transfers between devices  78.7 us (10%)
  other arithmetic  74.6 us (10%)
  blocking collectives  51.3 us (7%)
  starting transfers between devices  35.3 us (5%)
    gather x6, local copies, waits for them, and re-layouts, take_rows(): return jnp.take(row_table, row_ids, axis=0, mode='fill', fill_value=0)  233 us
    all_to_all x2, waiting for transfers between devices, combine(): lax.all_to_all(buf_rows, 'expert', 0, 0)  62.3 us
    all_to_all x1, blocking collectives, dispatch(): return lax.all_to_all(send_buf, 'expert', 0, 0)  51.3 us
    select_n x6, other arithmetic, take_rows(): return jnp.take(row_table, row_ids, axis=0, mode='fill', fill_value=0)  41 us
    dot_general x1, matrix products, expert_backward(): jnp.einsum('pecd,efd->pecf', d_buf, w_out, preferred_element_type=jnp.flo...  39.3 us
    scatter x1, local copies, waits for them, and re-layouts, slot_tables(): jnp.full((n_exp * capacity,), n_slot, jnp.int32).at[buf_pos]  30.9 us
    dot_general x1, matrix products, expert_backward(): jnp.einsum('pecf,pecd->efd', hidden, d_buf, preferred_element_type=jnp.fl...  26.1 us
    reshape x4, local copies, waits for them, and re-layouts, dispatch(): take_rows(row_src, row_ids).reshape(n_dev, n_local, capacity, model_dim)  21.1 us
  transfers between devices with their start and end apart: 9, of which 6 were waited for; matrix products, arithmetic and copies ran while one was open for 26% of the time, Pallas kernels for 0%

commit v1 on v0

v1 whole, which is shorter than its diff:
```python
import functools

import jax
import jax.numpy as jnp
from jax import lax
from jax.experimental import pallas as pl
from jax.experimental.pallas import tpu as pltpu
from jax.sharding import PartitionSpec as P

F32, BF16 = jnp.float32, jnp.bfloat16
NT = (((1,), (1,)), ((), ()))
ROW_TILE = 512
TOK_TILE = 512


def dot(a, b):
    return jnp.dot(a, b, preferred_element_type=F32)


def dot_nt(a, b):
    return lax.dot_general(a, b, NT, preferred_element_type=F32)


def sigmoid(a):
    return 0.5 + 0.5 * jnp.tanh(0.5 * a)


def local_kernel(xf_ref, xb_ref, dy_ref, gate_ref, w1_ref, w3_ref, w2_ref, y_ref, dx_ref, y_acc, dx_acc):
    e = pl.program_id(0)
    n_tok, model_dim = xf_ref.shape

    @pl.when(e == 0)
    def _():
        y_acc[...] = jnp.zeros_like(y_acc)
        dx_acc[...] = jnp.zeros_like(dx_acc)

    def tile(r, _):
        rows = pl.ds(pl.multiple_of(r * ROW_TILE, ROW_TILE), ROW_TILE)
        gate = jnp.broadcast_to(gate_ref[0, :, rows], (model_dim, ROW_TILE)).T
        w1, w3, w2 = w1_ref[0], w3_ref[0], w2_ref[0]
        a1, a3 = dot(xf_ref[rows], w1), dot(xf_ref[rows], w3)
        h = (a1 * sigmoid(a1) * a3).astype(BF16)
        y_acc[rows] += gate * dot(h, w2).astype(BF16).astype(F32)
        d = (gate * dy_ref[rows].astype(F32)).astype(BF16)
        b1, b3 = dot(xb_ref[rows], w1), dot(xb_ref[rows], w3)
        dh = dot_nt(d, w2).astype(BF16).astype(F32)
        sg = sigmoid(b1)
        act = b1 * sg
        d3 = (dh * act).astype(BF16)
        d1 = (dh * b3 * (sg + act * (1.0 - sg))).astype(BF16)
        dx_acc[rows] += (dot_nt(d1, w1) + dot_nt(d3, w3)).astype(BF16).astype(F32)
        return 0

    lax.fori_loop(0, n_tok // ROW_TILE, tile, 0)

    @pl.when(e == pl.num_programs(0) - 1)
    def _():
        y_ref[...] = y_acc[...].astype(BF16)
        dx_ref[...] = dx_acc[...].astype(BF16)


def owner_kernel(x_ref, dy_ref, gate_ref, w1_ref, w3_ref, w2_ref, g1_ref, g3_ref, g2_ref, w1t, w3t, acc1, acc3, acc2):
    i = pl.program_id(0)
    n_local = w1_ref.shape[0]

    @pl.when(i == 0)
    def _():
        for e in range(n_local):
            w1t[e] = w1_ref[e].T
            w3t[e] = w3_ref[e].T
        acc1[...] = jnp.zeros_like(acc1)
        acc3[...] = jnp.zeros_like(acc3)
        acc2[...] = jnp.zeros_like(acc2)

    x_t = x_ref[...].T
    dy_t = dy_ref[...].astype(F32).T

    def expert(e, _):
        d_t = (gate_ref[e] * dy_t).astype(BF16)
        a1, a3 = dot(w1t[e], x_t), dot(w3t[e], x_t)
        dh = dot(w2_ref[e], d_t).astype(BF16).astype(F32)
        sg = sigmoid(a1)
        act = a1 * sg
        h = (act * a3).astype(BF16)
        d3 = (dh * act).astype(BF16)
        d1 = (dh * a3 * (sg + act * (1.0 - sg))).astype(BF16)
        acc1[e] += dot_nt(d1, x_t)
        acc3[e] += dot_nt(d3, x_t)
        acc2[e] += dot_nt(h, d_t)
        return 0

    lax.fori_loop(0, n_local, expert, 0)

    @pl.when(i == pl.num_programs(0) - 1)
    def _():
        for e in range(n_local):
            g1_ref[e] = acc1[e].T.astype(BF16)
            g3_ref[e] = acc3[e].T.astype(BF16)
            g2_ref[e] = acc2[e].astype(BF16)


def local_call(x_f, x_b, dy, gates, w1, w3, w2):
    n_tok, model_dim = x_f.shape
    n_exp, _, ffn = w1.shape
    whole = pl.BlockSpec((n_tok, model_dim), lambda e: (0, 0))
    return pl.pallas_call(
        local_kernel,
        grid=(n_exp,),
        in_specs=[whole, whole, whole, pl.BlockSpec((1, 1, n_tok), lambda e: (e, 0, 0)), pl.BlockSpec((1, model_dim, ffn), lambda e: (e, 0, 0)), pl.BlockSpec((1, model_dim, ffn), lambda e: (e, 0, 0)), pl.BlockSpec((1, ffn, model_dim), lambda e: (e, 0, 0))],
        out_specs=[whole, whole],
        out_shape=[jax.ShapeDtypeStruct((n_tok, model_dim), BF16)] * 2,
        scratch_shapes=[pltpu.VMEM((n_tok, model_dim), F32)] * 2,
        cost_estimate=pl.CostEstimate(flops=16 * n_tok * n_exp * model_dim * ffn, bytes_accessed=8 << 20, transcendentals=0),
        compiler_params=pltpu.CompilerParams(vmem_limit_bytes=56 << 20),
        name='local_rows',
    )(x_f, x_b, dy, gates[:, None, :], w1, w3, w2)


def owner_call(x_all, dy_all, gates, w1, w3, w2):
    n_tok, model_dim = x_all.shape
    n_local, _, ffn = w1.shape
    toks = pl.BlockSpec((TOK_TILE, model_dim), lambda i: (i, 0))
    w_in = pl.BlockSpec((n_local, model_dim, ffn), lambda i: (0, 0, 0))
    w_out = pl.BlockSpec((n_local, ffn, model_dim), lambda i: (0, 0, 0))
    return pl.pallas_call(
        owner_kernel,
        grid=(n_tok // TOK_TILE,),
        in_specs=[toks, toks, pl.BlockSpec((n_local, 1, TOK_TILE), lambda i: (0, 0, i)), w_in, w_in, w_out],
        out_specs=[w_in, w_in, w_out],
        out_shape=[jax.ShapeDtypeStruct(w1.shape, BF16), jax.ShapeDtypeStruct(w3.shape, BF16), jax.ShapeDtypeStruct(w2.shape, BF16)],
        scratch_shapes=[pltpu.VMEM((n_local, ffn, model_dim), BF16)] * 2 + [pltpu.VMEM((n_local, ffn, model_dim), F32)] * 3,
        cost_estimate=pl.CostEstimate(flops=12 * n_tok * n_local * model_dim * ffn, bytes_accessed=8 << 20, transcendentals=0),
        compiler_params=pltpu.CompilerParams(vmem_limit_bytes=56 << 20),
        name='owner_grads',
    )(x_all, dy_all, gates, w1, w3, w2)


def solution(mesh):
    n_stage = mesh.shape['stage']
    n_dev = mesh.shape['expert']
    to_next = [(i, (i + 1) % n_stage) for i in range(n_stage)]
    to_prev = [((i + 1) % n_stage, i) for i in range(n_stage)]
    tok_spec = P('stage', 'expert', None)
    w_spec = P('stage', 'expert', None, None)

    def moe_layer(x_act, route_idx, route_wts, w_one, w_three, w_two, dy_act):
        x_src, dy = x_act[0], dy_act[0]
        n_tok = x_src.shape[0]
        n_local = w_one.shape[1]
        n_exp = n_local * n_dev
        w1, w3, w2 = w_one[0], w_three[0], w_two[0]

        idx = lax.ppermute(route_idx[0].T, 'stage', to_next)
        wts = lax.ppermute(route_wts[0].T, 'stage', to_next)
        x_f = lax.ppermute(x_src, 'stage', to_next)
        x_again, x_f = lax.optimization_barrier((x_src, x_f))
        x_b = lax.ppermute(x_again, 'stage', to_next)

        hit = idx[None, :, :] == jnp.arange(n_exp, dtype=jnp.int32)[:, None, None]
        gates = jnp.sum(jnp.where(hit, wts[None], 0.0), axis=1)
        my_gates = lax.all_to_all(gates.reshape(n_dev, n_local, n_tok), 'expert', 0, 0)
        my_gates = jnp.transpose(my_gates, (1, 0, 2)).reshape(n_local, 1, n_dev * n_tok)

        gather = functools.partial(lax.all_gather, axis_name='expert', axis=0, tiled=True)
        dy_all, x_all = gather(dy), gather(x_b)
        w1_all, w3_all, w2_all = gather(w1), gather(w3), gather(w2)

        g_one, g_three, g_two = owner_call(x_all, dy_all, my_gates, w1, w3, w2)
        y, dx = local_call(x_f, x_b, dy, gates, w1_all, w3_all, w2_all)
        dx_src = lax.ppermute(dx, 'stage', to_prev)
        return y[None], dx_src[None], g_one[None], g_three[None], g_two[None]

    return jax.shard_map(moe_layer, mesh=mesh, in_specs=(tok_spec, tok_spec, tok_spec, w_spec, w_spec, w_spec, tok_spec), out_specs=(tok_spec, tok_spec, w_spec, w_spec, w_spec), check_vma=False)
```

time: 767 us -> 334 us (0.44)
  local copies, waits for them, and re-layouts: 340 us -> 3.3 us
  Pallas kernels: 0 us -> 197 us
  matrix products: 178 us -> 0 us
  other arithmetic: 74.6 us -> 0.05 us
  blocking collectives: 51.3 us -> 7.36 us
  starting transfers between devices: 35.3 us -> 11.5 us
  waiting for transfers between devices: 78.7 us -> 94.8 us
  between operations: 1.19 us -> 13.8 us
    gather x6 -> x0, local copies, waits for them, and re-layouts: 233 us -> none  [take_rows(): return jnp.take(row_table, row_ids, axis=0, mode='fill', fill_value=0)]
    pallas_call x0 -> x2, Pallas kernels: none -> 197 us  [the longest x1 110 us: local_call(): pl.pallas_call(local_kernel, grid=(n_exp,), in_specs=[whole, whole, whole...]
    dot_general x10 -> x0, matrix products: 178 us -> none  [the longest x1 39.3 us: expert_backward(): jnp.einsum('pecd,efd->pecf', d_buf, w_out, preferred_element_type=jnp.flo...]
    all_gather x0 -> x5, waiting for transfers between devices: none -> 85.1 us  [the longest x3 85.1 us: moe_layer(): w1_all, w3_all, w2_all = (gather(w1), gather(w3), gather(w2))]
    all_to_all x4 -> x0, waiting for transfers between devices: 70.6 us -> none  [the longest x2 62.3 us: combine(): lax.all_to_all(buf_rows, 'expert', 0, 0)]
    all_to_all x1, blocking collectives: 51.3 us -> 7.36 us  [moe_layer(): lax.all_to_all(gates.reshape(n_dev, n_local, n_tok), 'expert', 0, 0)]
    select_n x7 -> x0, other arithmetic: 41.1 us -> none  [the longest x6 41 us: take_rows(): return jnp.take(row_table, row_ids, axis=0, mode='fill', fill_value=0)]
    scatter x1 -> x0, local copies, waits for them, and re-layouts: 30.9 us -> none  [slot_tables(): jnp.full((n_exp * capacity,), n_slot, jnp.int32).at[buf_pos]]
  transfers between devices with their start and end apart: 9 -> 10, of which waited for: 6 -> 6; matrix products, arithmetic and copies ran while one was open for 26% -> 1% of each run, Pallas kernels for 0% -> 33%
where the time goes in v1:
time: 334 us; the launch traced here: 328 us
  Pallas kernels  197 us (59%)
  waiting for transfers between devices  94.8 us (28%)
  between operations  13.8 us (4%)
  starting transfers between devices  11.5 us (3%)
  blocking collectives  7.36 us (2%)
    pallas_call x1, Pallas kernels, local_call(): pl.pallas_call(local_kernel, grid=(n_exp,), in_specs=[whole, whole, whole...  110 us
    pallas_call x1, Pallas kernels, owner_call(): pl.pallas_call(owner_kernel, grid=(n_tok // TOK_TILE,), in_specs=[toks, t...  87.6 us
    all_gather x3, waiting for transfers between devices, moe_layer(): w1_all, w3_all, w2_all = (gather(w1), gather(w3), gather(w2))  85.1 us
    all_to_all x1, blocking collectives, moe_layer(): lax.all_to_all(gates.reshape(n_dev, n_local, n_tok), 'expert', 0, 0)  7.36 us
  transfers between devices with their start and end apart: 10, of which 6 were waited for; matrix products, arithmetic and copies ran while one was open for 1% of the time, Pallas kernels for 33%

profile of v1, /device:TPU:113, one launch (start us, length us, event | category | flops | bytes accessed | tf_op | source)
XLA Modules:
  0.0 328.0 jit_solution(2616031299127543655)
XLA Ops:
  7.2 0.0 copy-start.1
  7.2 0.0 copy-start.3
  7.2 0.0 copy-start.4
  7.2 0.0 all-gather.16.cloned.1.call-start
  7.2 0.7 all-gather.16.cloned.1.call-update
  7.9 0.0 all-gather.12.cloned.1.call-start
  8.0 0.7 all-gather.12.cloned.1.call-update
  8.7 0.0 all-gather.14.cloned.1.call-start
  8.7 0.7 all-gather.14.cloned.1.call-update
  9.4 0.0 all-gather.18.cloned.1.call-start
  9.5 0.5 all-gather.18.cloned.1.call-update
  10.0 0.0 all-gather.10.cloned.1.call-start
  10.0 0.0 copy-done.1
  10.0 1.6 collective-permute-start
  11.7 6.1 %collective-permute-done.xf_ref = bf16[2048,128]{1,0:T(8,128)(2,1)S(1)} collective-permute-done((bf16[2048,128]{1,0:T(8,128)(2,1)S(1)}, bf16[2048,128]{1,0:T(8,128)(2,1)S(1)}, u32[]{:S(2)}, u32[]{:S(2)}) %collective-permute-start) | collective-permute-done | bytes 524320 | tf_op jit(solution)/shard_map/ppermute | solution.py:155
  17.8 0.0 copy-start.2
  17.8 2.5 collective-permute-start.1
  20.3 0.0 copy-done.3
  20.3 0.4 collective-permute-start.2
  20.7 0.0 copy-done.4
  20.7 5.8 %collective-permute-start.3 = (f32[4,2048]{1,0:T(4,128)S(1)}, f32[4,2048]{1,0:T(4,128)S(1)}, u32[]{:S(2)}, u32[]{:S(2)}) collective-permute-start(f32[4,2048]{1,0:T(4,128)S(1)} %bitcast.40), channel_id=1, source_target_pairs={{0,4},{4,8},{8,12},{12,16},{16,20},{20,24},{24,28},{28,32},{32,36}... | collective-permute-start | bytes 98312 | tf_op jit(solution)/shard_map/ppermute | solution.py:154
  26.5 0.2 collective-permute-done.2
  26.8 0.8 collective-permute-done.3
  27.5 0.1 select_reduce_fusion
  27.6 0.7 broadcast_in_dim.35.gate_ref
  28.4 0.0 collective-permute-done.1.xb_ref
  28.4 0.0 copy-start
  28.4 0.8 copy-done
  29.1 0.0 all-gather.10.cloned.1.call-update
  29.2 15.2 %all-gather.16.cloned.1.call-done = bf16[1,16,512,128]{3,2,0,1:T(8,128)(2,1)} async-done(((bf16[1,4,512,128]{3,2,0,1:T(8,128)(2,1)}), bf16[1,16,512,128]{3,2,0,1:T(8,128)(2,1)}) %all-gather.16.cloned.1.call-update) | async-done | bytes 2097168 | tf_op jit(solution)/shard_map/all_gather | solution.py:166
  44.3 34.9 %all-gather.12.cloned.1.call-done = bf16[1,16,128,512]{3,2,0,1:T(8,128)(2,1)} async-done(((bf16[1,4,128,512]{3,2,0,1:T(8,128)(2,1)}), bf16[1,16,128,512]{3,2,0,1:T(8,128)(2,1)}) %all-gather.12.cloned.1.call-update) | async-done | bytes 2097168 | tf_op jit(solution)/shard_map/all_gather | solution.py:166
  79.3 35.0 %all-gather.14.cloned.1.call-done = bf16[1,16,128,512]{3,2,0,1:T(8,128)(2,1)} async-done(((bf16[1,4,128,512]{3,2,0,1:T(8,128)(2,1)}), bf16[1,16,128,512]{3,2,0,1:T(8,128)(2,1)}) %all-gather.14.cloned.1.call-update) | async-done | bytes 2097168 | tf_op jit(solution)/shard_map/all_gather | solution.py:166
  114.3 0.0 copy-done.2
  114.3 109.5 %local_rows.1 = (bf16[2048,128]{1,0:T(8,128)(2,1)}, bf16[2048,128]{1,0:T(8,128)(2,1)}) custom-call(bf16[2048,128]{1,0:T(8,128)(2,1)} %copy-done.2, bf16[2048,128]{1,0:T(8,128)(2,1)} %copy-done, bf16[2048,128]{1,0:T(8,128)(2,1)} %bitcast.24, f32[16,1,2048]{2,1,0:T(1,128)} %broadcast_in_dim.35.gate_ref, bf16[16,128,512]{2,1,0:T(8,128)(2,1)} %bitcast.35, ...), custom_call_target="tpu_custom_call" | custom-call | flops 34359738368 | bytes 8388608 | tf_op jit(solution)/shard_map/local_rows/pallas_call | solution.py:106
  223.8 0.9 collective-permute-start.4
  224.7 7.4 %all_to_all.5 = f32[4,4,2048]{2,1,0:T(4,128)S(1)} all-to-all(f32[4,4,2048]{2,1,0:T(4,128)S(1)} %reshape.18), channel_id=1, replica_groups=mesh['stage'=64,'expert'=4] {'expert'}, dimensions={0} | all-to-all | bytes 262144 | tf_op jit(solution)/shard_map/all_to_all | solution.py:161
  232.1 0.1 copy.20
  232.2 0.8 reshape.19.gate_ref
  233.0 0.0 collective-permute-done.4
  233.0 0.0 all-gather.18.cloned.1.call-done
  233.0 0.0 all-gather.10.cloned.1.call-done.x_ref
  233.0 87.6 %owner_grads.1 = (bf16[4,128,512]{2,1,0:T(8,128)(2,1)}, bf16[4,128,512]{2,1,0:T(8,128)(2,1)}, bf16[4,512,128]{2,1,0:T(8,128)(2,1)}) custom-call(bf16[8192,128]{1,0:T(8,128)(2,1)} %all-gather.10.cloned.1.call-done.x_ref, bf16[8192,128]{1,0:T(8,128)(2,1)} %bitcast.33, f32[4,1,8192]{2,1,0:T(1,128)} %reshape.19.gate_ref, bf16[4,128,512]{2,1,0:T(8,128)(2,1)} %bitcast.28, ...), custom_call_target="tpu_custom_call" | custom-call | flops 25769803776 | bytes 8388608 | tf_op jit(solution)/shard_map/owner_grads/pallas_call | solution.py:125
  320.7 0.8 copy.22
  (1 shorter events, 0.0 us)
Async XLA Ops:
  7.2 2.9 copy-start.1
  7.2 13.1 %copy-start.3 = (s32[1,2048,4]{1,2,0:T(4,128)S(1)}, s32[1,2048,4]{1,2,0:T(4,128)}, u32[]{:S(2)}) copy-start(s32[1,2048,4]{1,2,0:T(4,128)} %param.8) | copy-start | bytes 98308
  7.2 13.5 %copy-start.4 = (f32[1,2048,4]{1,2,0:T(4,128)S(1)}, f32[1,2048,4]{1,2,0:T(4,128)}, u32[]{:S(2)}) copy-start(f32[1,2048,4]{1,2,0:T(4,128)} %param.9) | copy-start | bytes 98308
  7.2 37.2 %all-gather.16.cloned.1.call-start = ((), (), s32[]{:S(2)}) async-start(), calls=%async_computation.4 | async-start | bytes 2621440 | tf_op jit(solution)/shard_map/all_gather | solution.py:166
  7.9 71.4 %all-gather.12.cloned.1.call-start = ((), (), s32[]{:S(2)}) async-start(), calls=%async_computation.2 | async-start | bytes 2621440 | tf_op jit(solution)/shard_map/all_gather | solution.py:166
  8.7 105.6 %all-gather.14.cloned.1.call-start = ((), (), s32[]{:S(2)}) async-start(), calls=%async_computation.3 | async-start | bytes 2621440 | tf_op jit(solution)/shard_map/all_gather | solution.py:166
  9.4 223.6 %all-gather.18.cloned.1.call-start = ((), (), s32[]{:S(2)}) async-start(), calls=%async_computation.5 | async-start | bytes 2621440 | tf_op jit(solution)/shard_map/all_gather | solution.py:165
  10.0 223.0 %all-gather.10.cloned.1.call-start = ((), (), s32[]{:S(2)}) async-start(), calls=%async_computation.1 | async-start | bytes 2621440 | tf_op jit(solution)/shard_map/all_gather | solution.py:165
  10.0 7.7 %collective-permute-start = (bf16[2048,128]{1,0:T(8,128)(2,1)S(1)}, bf16[2048,128]{1,0:T(8,128)(2,1)S(1)}, u32[]{:S(2)}, u32[]{:S(2)}) collective-permute-start(bf16[2048,128]{1,0:T(8,128)(2,1)S(1)} %bitcast.37), channel_id=1, source_target_pairs={{0,4},{4,8},{8,12},{12,16},{16,20},{20,24},{24,28},{28,32},{32,36}... | collective-permute-start | bytes 1572872 | tf_op jit(solution)/shard_map/ppermute | solution.py:155
  17.8 96.5 %copy-start.2 = (bf16[2048,128]{1,0:T(8,128)(2,1)}, bf16[2048,128]{1,0:T(8,128)(2,1)S(1)}, u32[]{:S(2)}) copy-start(bf16[2048,128]{1,0:T(8,128)(2,1)S(1)} %collective-permute-done.xf_ref) | copy-start | bytes 1572868
  17.8 10.6 %collective-permute-start.1 = (bf16[2048,128]{1,0:T(8,128)(2,1)S(1)}, bf16[2048,128]{1,0:T(8,128)(2,1)S(1)}, u32[]{:S(2)}, u32[]{:S(2)}) collective-permute-start(bf16[2048,128]{1,0:T(8,128)(2,1)S(1)} %bitcast.38), channel_id=1, source_target_pairs={{0,4},{4,8},{8,12},{12,16},{16,20},{20,24},{24,28},{28,32},{32,36}... | collective-permute-start | bytes 1572872 | tf_op jit(solution)/shard_map/ppermute | solution.py:157
  20.3 6.5 %collective-permute-start.2 = (s32[4,2048]{1,0:T(4,128)S(1)}, s32[4,2048]{1,0:T(4,128)S(1)}, u32[]{:S(2)}, u32[]{:S(2)}) collective-permute-start(s32[4,2048]{1,0:T(4,128)S(1)} %bitcast.39), channel_id=1, source_target_pairs={{0,4},{4,8},{8,12},{12,16},{16,20},{20,24},{24,28},{28,32},{32,36}... | collective-permute-start | bytes 98312 | tf_op jit(solution)/shard_map/ppermute | solution.py:153
  20.7 6.8 %collective-permute-start.3 = (f32[4,2048]{1,0:T(4,128)S(1)}, f32[4,2048]{1,0:T(4,128)S(1)}, u32[]{:S(2)}, u32[]{:S(2)}) collective-permute-start(f32[4,2048]{1,0:T(4,128)S(1)} %bitcast.40), channel_id=1, source_target_pairs={{0,4},{4,8},{8,12},{12,16},{16,20},{20,24},{24,28},{28,32},{32,36}... | collective-permute-start | bytes 98312 | tf_op jit(solution)/shard_map/ppermute | solution.py:154
  28.4 0.8 copy-start
  223.8 9.3 %collective-permute-start.4 = (bf16[2048,128]{1,0:T(8,128)(2,1)}, bf16[2048,128]{1,0:T(8,128)(2,1)S(1)}, u32[]{:S(2)}, u32[]{:S(2)}) collective-permute-start(bf16[2048,128]{1,0:T(8,128)(2,1)} %get-tuple-element.15), channel_id=1, source_target_pairs={{4,0},{8,4},{12,8},{16,12},{20,16},{24,20},{28,24},{32,28},{36,32}... | collective-permute-start | bytes 1572872 | tf_op jit(solution)/shard_map/ppermute | solution.py:170
Sparse Core Ops, SparseCore 0:
  9.8 34.4 all-gather.15
  46.2 33.0 all-gather.11
  81.1 33.0 all-gather.13
  115.9 33.0 all-gather.17
  151.3 33.1 all-gather.9
